TPU v7x, 32 devices: a whole 2x2x4 slice. The times are simulated.
32 devices in a mesh: col: 32 (over z, y, x, core).
Axes of the slice: x: 2, y: 2, z: 4, core: 2. Of those that a mesh axis runs over, the one named last changes fastest.
Arguments:
- matrix: float32 [4096, 4096], P(None, 'col'), as said below
- rhs_rows: float32 [2048, 4096], P('col'), may hold values from -6 to 6
Outputs:
- eliminated: float32 [4096, 4096], P(None, 'col')
- solved_rows: float32 [2048, 4096], P('col')
Inputs may be any that keep to these rules, and one draw needn't show every extreme that they name: `matrix`: the diagonal entries lie between 1.5 * sqrt(4096) and 3 * sqrt(4096); the other entries between -4 and 4.
All inputs are finite; a program needn't handle non-finite values.
Results may differ from a plain program's by a relative error of at most 0.0001.
Values sent between devices are 32-bit elements; how exact they have to be, the bound alone decides.
No kernel may reach another device: no remote copies, remote signals or barrier semaphores. Data moves between devices by JAX's collectives and lax.ppermute only.
A program may use at most 192 MiB of HBM per device.

v0:
```python
import jax
import jax.numpy as jnp
from jax import lax
from jax.sharding import PartitionSpec as P

BLK = 128
BLK_DEV = 1
STEPS = 2


def broadcast(value, axis, source):
    kept = jnp.where(lax.axis_index(axis) == source, value, 0).astype(value.dtype)
    return lax.psum(kept, axis)


def pivot_inverse(pivot_block):
    gram = jnp.dot(
        pivot_block.T,
        pivot_block,
        precision=lax.Precision.HIGHEST,
        preferred_element_type=jnp.float32,
    )
    lower = jnp.linalg.cholesky(gram)
    return jax.scipy.linalg.cho_solve((lower, True), pivot_block.T)


def unchanged(local_cols):
    return local_cols


def body(matrix, rhs_rows):
    precise = lax.Precision.HIGHEST
    own_index = lax.axis_index("col")
    fetched = []
    for step in range(STEPS):
        fetched.append(broadcast(matrix, "col", step))
    for step in range(STEPS):
        row_start = step * BLK_DEV * BLK
        row_end = row_start + BLK
        panel_cols = fetched[step]
        inverse = pivot_inverse(panel_cols[row_start:row_end])
        scaled = jnp.dot(
            inverse,
            matrix[row_start:row_end],
            precision=precise,
            preferred_element_type=jnp.float32,
        )
        matrix = matrix - jnp.dot(
            panel_cols, scaled, precision=precise, preferred_element_type=jnp.float32
        )
        matrix = matrix.at[row_start:row_end].set(scaled)

        def place_column(local_cols):
            column = -jnp.dot(
                panel_cols, inverse, precision=precise, preferred_element_type=jnp.float32
            )
            column = column.at[row_start:row_end].set(inverse)
            return local_cols.at[:, :BLK].set(column)

        matrix = lax.cond(own_index == step, place_column, unchanged, matrix)
        solved = jnp.dot(
            rhs_rows[:, row_start:row_end],
            inverse.T,
            precision=precise,
            preferred_element_type=jnp.float32,
        )
        rhs_rows = rhs_rows - jnp.dot(
            solved, panel_cols.T, precision=precise, preferred_element_type=jnp.float32
        )
        rhs_rows = rhs_rows.at[:, row_start:row_end].set(solved)
        for later in range(step + 1, STEPS):
            row_part = jnp.dot(
                inverse,
                fetched[later][row_start:row_end],
                precision=precise,
                preferred_element_type=jnp.float32,
            )
            updated = fetched[later] - jnp.dot(
                panel_cols, row_part, precision=precise, preferred_element_type=jnp.float32
            )
            fetched[later] = updated.at[row_start:row_end].set(row_part)
    return (matrix, rhs_rows)


def solution(mesh):
    return jax.shard_map(
        body,
        mesh=mesh,
        in_specs=(P(None, "col"), P("col", None)),
        out_specs=(P(None, "col"), P("col", None)),
        check_vma=False,
    )
```

profile of v0, /device:TPU:0, one launch (start us, length us, event | category | flops | bytes accessed | tf_op | source)
XLA Modules:
  0.0 248.9 jit_solution(937625850335362420)
XLA Ops:
  7.2 0.0 all-reduce.3.cloned.1.call-start
  7.2 3.9 %broadcast_select_fusion = (f32[4096,128]{1,0:T(8,128)}, f32[4096,128]{1,0:T(8,128)}) fusion(f32[4096,128]{1,0:T(8,128)} %param.31, pred[]{:T(512)S(6)} %eq.8, pred[]{:T(512)S(6)} %eq.9), kind=kLoop, calls=%fused_computation.7 | loop fusion | flops 1048576 | bytes 6291458 | tf_op jit(solution)/shard_map/jit(_where)/select_n | solution.py:12
  11.1 0.0 all-reduce.3.cloned.1.call-update
  11.1 0.7 compare_reduce_fusion.3
  11.8 0.7 compare_reduce_fusion.2
  12.5 147.2 %all-reduce.3.cloned.1.call-done = (f32[4096,128]{1,0:T(8,128)}, f32[4096,128]{1,0:T(8,128)}) async-done(((f32[4096,128]{1,0:T(8,128)}, f32[4096,128]{1,0:T(8,128)}), (f32[4096,128]{1,0:T(8,128)}, f32[4096,128]{1,0:T(8,128)})) %all-reduce.3.cloned.1.call-update) | async-done | bytes 4194320 | tf_op jit(solution)/shard_map/psum | solution.py:13
  159.7 1.2 fusion.24
  160.9 0.1 copy.4
  161.0 11.7 %cholesky.44 = f32[128,128]{1,0:T(8,128)S(1)} custom-call(f32[128,128]{1,0:T(8,128)S(1)} %fusion.17), custom_call_target="Cholesky" | custom-call | tf_op jit(solution)/shard_map/jit(cholesky)/cholesky | solution.py:23
  172.7 0.6 compare_reduce_fusion.1
  173.4 0.7 fusion
  174.1 9.8 %custom-call.8 = f32[1,128,128]{1,2,0:T(8,128)S(1)} custom-call(f32[1,128,128]{2,1,0:T(8,128)S(1)} %fusion), custom_call_target="InvertDiagBlocksLowerTriangular" | custom-call | tf_op jit(solution)/shard_map/jit(_cho_solve)/triangular_solve | solution.py:24
  183.9 1.1 fusion.12
  185.0 0.2 fusion.14
  185.2 1.0 fusion.18
  186.3 0.0 copy-done.5
  186.3 0.2 fusion.30
  186.5 1.0 fusion.4
  187.6 4.2 %convolution_subtract_fusion = f32[4096,128]{1,0:T(8,128)S(1)} fusion(f32[4096,128]{1,0:T(8,128)} %get-tuple-element.213, f32[4096,128]{1,0:T(8,128)} %get-tuple-element.212, f32[128,128]{1,0:T(8,128)S(1)} %fusion.4), kind=kOutput, calls=%fused_computation.4 | convolution fusion | flops 805830656 | bytes 6356992 | tf_op jit(solution)/shard_map/dot_general | solution.py:78
  191.8 0.0 copy-start.1
  191.8 1.3 copy-done.1
  193.2 0.3 fusion.21
  193.4 0.1 copy.5
  193.6 11.8 %cholesky.55 = f32[128,128]{1,0:T(8,128)S(1)} custom-call(f32[128,128]{1,0:T(8,128)S(1)} %fusion.11), custom_call_target="Cholesky" | custom-call | tf_op jit(solution)/shard_map/jit(cholesky)/cholesky | solution.py:23
  205.4 0.6 compare_reduce_fusion
  206.1 0.6 fusion.1
  206.7 9.8 %custom-call.9 = f32[1,128,128]{1,2,0:T(8,128)S(1)} custom-call(f32[1,128,128]{2,1,0:T(8,128)S(1)} %fusion.1), custom_call_target="InvertDiagBlocksLowerTriangular" | custom-call | tf_op jit(solution)/shard_map/jit(_cho_solve)/triangular_solve | solution.py:24
  216.5 1.1 fusion.6
  217.7 0.2 fusion.8
  217.9 0.0 copy-start.2
  217.9 2.4 convolution_subtract_fusion.2
  220.3 0.6 fusion.29
  220.9 0.2 fusion.27
  221.2 2.4 convolution_subtract_fusion.1
  223.6 0.0 copy-start.4
  223.6 1.8 fusion.32
  225.5 3.7 %conditional.2 = (f32[4096,128]{1,0:T(8,128)}) conditional(s32[]{:T(128)} %convert_element_type.10, (f32[4096,128]{1,0:T(8,128)S(1)}, f32[4096,128]{1,0:T(8,128)S(1)}, f32[128,128]{1,0:T(8,128)S(1)}) %tuple.107, (f32[4096,128]{1,0:T(8,128)S(1)}, f32[128,128]{1,0:T(8,128)S(1)}) %tuple.105), branch_computations={%region_3.6_spmd, %region_4.7_spmd} | conditional | flops 805830656 | bytes 6422536 | solution.py:60
  225.5 3.1 %convolution_negate_fusion = f32[4096,128]{1,0:T(8,128)} fusion(f32[4096,128]{1,0:T(8,128)S(1)} %get-tuple-element.197, f32[128,128]{1,0:T(8,128)S(1)} %get-tuple-element.198), kind=kOutput, calls=%fused_computation.1 | convolution fusion | flops 805830656 | bytes 4259840 | tf_op jit(solution)/shard_map/cond/branch_1_fun/dot_general | solution.py:54
  228.6 0.6 constant_dynamic-update-slice_fusion.1
  229.2 1.0 fusion.2
  230.2 0.0 copy-start.3
  230.3 4.9 %fusion.33 = f32[4096,128]{1,0:T(8,128)} fusion(f32[4096,128]{1,0:T(8,128)} %copy-done.1, f32[128,128]{1,0:T(8,128)S(1)} %fusion.2), kind=kOutput, calls=%fused_computation.58 | convolution fusion | flops 805306368 | bytes 4259840 | tf_op jit(solution)/shard_map/dot_general | solution.py:48
  235.1 0.6 fusion.26
  235.8 0.0 copy-start.6
  235.8 1.0 copy-done.6
  236.8 3.8 %conditional.3 = (f32[4096,128]{1,0:T(8,128)}, f32[128,128]{1,0:T(8,128)S(1)}, s32[]{:T(128)}) conditional(s32[]{:T(128)} %convert_element_type.9, (f32[4096,128]{1,0:T(8,128)}, f32[4096,128]{1,0:T(8,128)}, f32[128,128]{1,0:T(8,128)S(1)}) %tuple.94, (f32[4096,128]{1,0:T(8,128)S(1)}, f32[128,128]{1,0:T(8,128)S(1)}) %tuple.106), branch_computations={%region_6.0_spmd, %region_7.10_spmd} | conditional | flops 805830656 | bytes 6291488 | solution.py:60
  236.8 3.8 %sub.15 = f32[4096,128]{1,0:T(8,128)} subtract(f32[4096,128]{1,0:T(8,128)} %get-tuple-element.199, f32[4096,128]{1,0:T(8,128)} %get-tuple-element.200) | non-fusion elementwise | flops 524288 | bytes 6291456 | tf_op jit(solution)/shard_map/sub | solution.py:48
  240.5 1.5 scatter.30
  (11 shorter events, 0.1 us)
Async XLA Ops:
  7.2 152.5 %all-reduce.3.cloned.1.call-start = ((), (), s32[]{:S(2)}) async-start(), calls=%async_computation | async-start | bytes 8388608 | tf_op jit(solution)/shard_map/psum | solution.py:13
  11.1 175.2 %copy-start.5 = (f32[64,4096]{1,0:T(8,128)S(1)}, f32[64,4096]{1,0:T(8,128)}, u32[]{:S(2)}) copy-start(f32[64,4096]{1,0:T(8,128)} %param.32) | copy-start | bytes 3145732
  187.6 30.3 %copy-start = (f32[4096,128]{1,0:T(8,128)S(1)}, f32[4096,128]{1,0:T(8,128)}, u32[]{:S(2)}) copy-start(f32[4096,128]{1,0:T(8,128)} %get-tuple-element.212) | copy-start | bytes 6291460
  191.8 1.3 copy-start.1
  217.9 3.3 %copy-start.2 = (f32[4096,128]{1,0:T(8,128)S(1)}, f32[4096,128]{1,0:T(8,128)}, u32[]{:S(2)}) copy-start(f32[4096,128]{1,0:T(8,128)} %copy-done.1) | copy-start | bytes 6291460
  223.6 1.9 copy-start.4
  230.2 4.9 %copy-start.3 = (f32[4096,128]{1,0:T(8,128)S(1)}, f32[4096,128]{1,0:T(8,128)}, u32[]{:S(2)}) copy-start(f32[4096,128]{1,0:T(8,128)} %copy-done.1) | copy-start | bytes 6291460
  235.8 1.0 copy-start.6
Sparse Core Ops, SparseCore 0:
  14.3 145.3 all-reduce.2
where the time goes:
time: 249 us
  waiting for transfers between devices  147 us (59%)
  other arithmetic  56.1 us (23%)
  matrix products  26.6 us (11%)
  between operations  14.3 us (6%)
  local copies, waits for them, and re-layouts  4.64 us (2%)
    psum x1, waiting for transfers between devices, broadcast(): return lax.psum(kept, axis)  147 us
    another operation x6, other arithmetic, pivot_inverse(): lower = jnp.linalg.cholesky(gram)  24.9 us
    another operation x4, other arithmetic, pivot_inverse(): return jax.scipy.linalg.cho_solve((lower, True), pivot_block.T)  20.9 us
    dot_general x2, matrix products, body(): jnp.dot(panel_cols, scaled, precision=precise, preferred_element_type=jnp...  6.72 us
  transfers between devices with their start and end apart: 1, of which 1 were waited for; matrix products, arithmetic and copies ran while one was open for 1% of the time, Pallas kernels for 0%

commit v1 on v0

--- a/solution.py
+++ b/solution.py
@@ -10,7 +10,7 @@
 
 def broadcast(value, axis, source):
     kept = jnp.where(lax.axis_index(axis) == source, value, 0).astype(value.dtype)
-    return lax.psum(kept, axis)
+    return jnp.sum(lax.all_gather(kept, axis), axis=0)
 
 
 def pivot_inverse(pivot_block):

time: 249 us -> 812 us (3.26)
  waiting for transfers between devices: 147 us -> 667 us
  other arithmetic: 56.1 us -> 101 us
    all_gather x0 -> x2, waiting for transfers between devices: none -> 666 us  [broadcast(): return jnp.sum(lax.all_gather(kept, axis), axis=0)]
    psum x1 -> x0, waiting for transfers between devices: 147 us -> none  [broadcast(): return lax.psum(kept, axis)]
    reduce_sum x0 -> x2, other arithmetic: none -> 45.3 us  [broadcast(): return jnp.sum(lax.all_gather(kept, axis), axis=0)]
  transfers between devices with their start and end apart: 1 -> 2, of which waited for: 1 -> 2; matrix products, arithmetic and copies ran while one was open for 1% -> 6% of each run, Pallas kernels for 0% -> 0%
where the time goes in v1:
time: 812 us; the launch traced here: 811 us
  waiting for transfers between devices  667 us (82%)
  other arithmetic  101 us (12%)
  matrix products  24.3 us (3%)
  between operations  14.3 us (2%)
    all_gather x2, waiting for transfers between devices, broadcast(): return jnp.sum(lax.all_gather(kept, axis), axis=0)  666 us
    reduce_sum x2, other arithmetic, broadcast(): return jnp.sum(lax.all_gather(kept, axis), axis=0)  45.3 us
    another operation x6, other arithmetic, pivot_inverse(): lower = jnp.linalg.cholesky(gram)  24.8 us
    another operation x4, other arithmetic, pivot_inverse(): return jax.scipy.linalg.cho_solve((lower, True), pivot_block.T)  20.9 us
  transfers between devices with their start and end apart: 2, of which 2 were waited for; matrix products, arithmetic and copies ran while one was open for 6% of the time, Pallas kernels for 0%

profile of v1, /device:TPU:0, one launch (start us, length us, event | category | flops | bytes accessed | tf_op | source)
XLA Modules:
  0.0 811.3 jit_solution(13815869645695718542)
XLA Ops:
  7.2 0.0 all-gather.5.cloned.1.call-start
  7.2 3.9 broadcast_select_fusion
  11.1 0.0 all-gather.5.cloned.1.call-update
  11.1 0.0 all-gather.7.cloned.1.call-start
  11.2 0.7 all-gather.7.cloned.1.call-update
  11.9 0.6 compare_reduce_fusion.3
  12.5 0.7 compare_reduce_fusion.2
  13.2 356.5 %all-gather.5.cloned.1.call-done = f32[131072,128]{1,0:T(8,128)} async-done(((f32[4096,128]{1,0:T(8,128)}), f32[131072,128]{1,0:T(8,128)}) %all-gather.5.cloned.1.call-update) | async-done | bytes 67108880 | tf_op jit(solution)/shard_map/all_gather | solution.py:13
  369.7 23.0 %reduce_sum.18 = f32[4096,128]{1,0:T(8,128)S(1)} reduce(f32[32,4096,128]{2,1,0:T(8,128)} %bitcast, f32[]{:T(128)} %constant.313.clone.1), dimensions={0}, to_apply=%region_0.1 | reduce | flops 16252928 | bytes 69206016 | tf_op jit(solution)/shard_map/reduce_sum | solution.py:13
  392.6 0.3 fusion.24
  392.9 0.1 copy.4
  393.1 11.7 %cholesky.44 = f32[128,128]{1,0:T(8,128)S(1)} custom-call(f32[128,128]{1,0:T(8,128)S(1)} %fusion.17), custom_call_target="Cholesky" | custom-call | tf_op jit(solution)/shard_map/jit(cholesky)/cholesky | solution.py:23
  404.8 0.6 compare_reduce_fusion.1
  405.4 0.6 fusion
  406.0 9.8 %custom-call.8 = f32[1,128,128]{1,2,0:T(8,128)S(1)} custom-call(f32[1,128,128]{2,1,0:T(8,128)S(1)} %fusion), custom_call_target="InvertDiagBlocksLowerTriangular" | custom-call | tf_op jit(solution)/shard_map/jit(_cho_solve)/triangular_solve | solution.py:24
  415.8 0.3 fusion.12
  416.1 0.2 fusion.14
  416.3 1.0 fusion.18
  417.4 309.6 %all-gather.7.cloned.1.call-done = f32[131072,128]{1,0:T(8,128)} async-done(((f32[4096,128]{1,0:T(8,128)}), f32[131072,128]{1,0:T(8,128)}) %all-gather.7.cloned.1.call-update) | async-done | bytes 67108880 | tf_op jit(solution)/shard_map/all_gather | solution.py:13
  727.0 22.3 %reduce_sum.19 = f32[4096,128]{1,0:T(8,128)} reduce(f32[32,4096,128]{2,1,0:T(8,128)} %bitcast.5, f32[]{:T(128)} %constant.313.clone.1), dimensions={0}, to_apply=%region_5.0 | reduce | flops 16252928 | bytes 69206016 | tf_op jit(solution)/shard_map/reduce_sum | solution.py:13
  749.3 0.2 fusion.30
  749.6 1.0 fusion.4
  750.6 3.5 convolution_subtract_fusion
  754.1 1.3 copy-done
  755.4 0.3 fusion.21
  755.7 0.1 copy.5
  755.8 11.7 %cholesky.55 = f32[128,128]{1,0:T(8,128)S(1)} custom-call(f32[128,128]{1,0:T(8,128)S(1)} %fusion.11), custom_call_target="Cholesky" | custom-call | tf_op jit(solution)/shard_map/jit(cholesky)/cholesky | solution.py:23
  767.6 0.7 compare_reduce_fusion
  768.3 0.7 fusion.1
  769.0 9.8 %custom-call.9 = f32[1,128,128]{1,2,0:T(8,128)S(1)} custom-call(f32[1,128,128]{2,1,0:T(8,128)S(1)} %fusion.1), custom_call_target="InvertDiagBlocksLowerTriangular" | custom-call | tf_op jit(solution)/shard_map/jit(_cho_solve)/triangular_solve | solution.py:24
  778.8 1.1 fusion.6
  780.0 0.2 fusion.8
  780.2 2.4 convolution_subtract_fusion.2
  782.6 0.6 fusion.29
  783.2 0.2 fusion.27
  783.4 2.6 convolution_subtract_fusion.1
  786.0 1.8 fusion.32
  787.9 3.7 conditional.2
  787.9 3.1 convolution_negate_fusion
  791.0 0.6 constant_dynamic-update-slice_fusion.1
  791.6 1.0 fusion.2
  792.7 4.9 fusion.33
  797.6 0.6 fusion.26
  798.2 0.0 copy-start.5
  798.2 1.0 copy-done.5
  799.2 3.8 conditional.3
  799.2 3.8 sub.15
  802.9 1.5 scatter.30
  (14 shorter events, 0.1 us)
Async XLA Ops:
  7.2 362.5 %all-gather.5.cloned.1.call-start = ((), (), s32[]{:S(2)}) async-start(), calls=%async_computation | async-start | bytes 69206016 | tf_op jit(solution)/shard_map/all_gather | solution.py:13
  11.1 715.8 %all-gather.7.cloned.1.call-start = ((), (), s32[]{:S(2)}) async-start(), calls=%async_computation.1 | async-start | bytes 69206016 | tf_op jit(solution)/shard_map/all_gather | solution.py:13
  727.0 22.4 %copy-start.4 = (f32[64,4096]{1,0:T(8,128)S(1)}, f32[64,4096]{1,0:T(8,128)}, u32[]{:S(2)}) copy-start(f32[64,4096]{1,0:T(8,128)} %param.32) | copy-start | bytes 3145732
  754.1 1.3 copy-start
  780.2 3.2 copy-start.1
  786.0 1.9 copy-start.3
  792.7 4.9 copy-start.2
  798.2 1.0 copy-start.5
Sparse Core Ops, SparseCore 0:
  11.3 358.3 all-gather.4
  373.1 353.8 all-gather.6
